TPU v7x, 128 devices: a whole 4x4x4 slice. The times are simulated.
128 devices in a mesh: dp: 16 (over z, x), mp: 8 (over y, core).
Axes of the slice: x: 4, y: 4, z: 4, core: 2. Of those that a mesh axis runs over, the one named last changes fastest.
Arguments:
- tokens: bfloat16 [256, 4096], P('dp'), may hold values from -6 to 6
- norm_gain: float32 [4096], replicated, may hold values from 0.5 to 1.5
- router: bfloat16 [4096, 8], replicated, may hold values from -0.09375 to 0.09375
- w_gate: bfloat16 [8, 4096, 14336], P('mp', None, 'dp'), may hold values from -0.09375 to 0.09375
- w_up: bfloat16 [8, 4096, 14336], P('mp', None, 'dp'), may hold values from -0.09375 to 0.09375
- w_down: bfloat16 [8, 14336, 4096], P('mp', 'dp'), may hold values from -0.046875 to 0.046875
- final_gain: float32 [4096], replicated, may hold values from 0.5 to 1.5
- routes: int32 [256, 2], replicated, may hold values from 0 to 7, all different within a row; in each aligned block of 16 rows (0 to 15, 16 to 31, ...) at most 8 rows name the same one
- steer_hidden: bfloat16 [2, 256, 1024], P(None, 'dp'), may hold values from -6 to 6
- steer_query: bfloat16 [2, 256, 1024], P(None, 'dp', 'mp'), may hold values from -200 to 200
- steer_cache: bfloat16 [2, 2, 256, 64, 1024], P(None, None, 'dp', None, 'mp'), may hold values from -6 to 6
- steer_new: bfloat16 [2, 2, 256, 1024], P(None, None, 'dp', 'mp'), may hold values from -6 to 6
- cache_len: int32 [256], P('dp'), may hold values from 1 to 64
- steer_out: bfloat16 [2, 1024, 1024], P(None, 'mp'), may hold values from -0.1875 to 0.1875
- steer_gain: float32 [2, 1024], replicated, may hold values from 0.5 to 1.5
- base_head: bfloat16 [4096, 16000], P(None, ('dp', 'mp')), may hold values from -0.09375 to 0.09375
- steer_head: bfloat16 [2, 1024, 16000], P(None, None, ('dp', 'mp')), may hold values from -0.1875 to 0.1875
- inv_temp: float32 [256], replicated, may hold values from 0.5 to 40
Outputs:
- log_probs: float32 [256, 16000], P(None, ('dp', 'mp'))
Inputs may be any that keep to these rules, and one draw needn't show every extreme that they name: The two routes of a sequence differ; in every aligned block of 16 sequences (the sequences of one index of dp) no expert is named more than 8 times. Positions at and after cache_len[s] of sequence s's cache are unused.
All inputs are finite; a program needn't handle non-finite values.
Results may differ from a plain program's by a relative error of at most 0.00105.
Values may be sent and summed in bfloat16 or wider, within the bound.
A program may use at most 128 MiB of HBM per device.

v0:
```python
import math
import jax
import jax.numpy as jnp
from jax import lax
from jax.sharding import Mesh
from jax.sharding import PartitionSpec as P

HEAD_DIM = 128
MP = ("mp_0", "mp_1")
DP = ("dp_0", "dp_1")
DP_MP = ("dp_0", "dp_1", "mp_0", "mp_1")
steer_alpha = 2.0
norm_eps = 1e-05


def copy_for_each(x, axis):
    size = lax.axis_size(axis)
    return lax.all_to_all(jnp.broadcast_to(x[None], (size, *x.shape)), axis, 0, 0, tiled=True)


def over_copies(x, axis):
    everything = copy_for_each(x, axis)
    return jnp.sum(everything, axis=0)


def in_order(blocks, dim):
    blocks = jnp.moveaxis(blocks, 0, dim)
    dims = blocks.shape
    return blocks.reshape(*dims[:dim], dims[dim] * dims[dim + 1], *dims[dim + 2 :])


def gathered_copies(x, axis, dim):
    return in_order(copy_for_each(x, axis), dim)


def cut_along(x, dim, size):
    dims = x.shape
    blocks = x.reshape(*dims[:dim], size, dims[dim] // size, *dims[dim + 1 :])
    return jnp.moveaxis(blocks, dim, 0)


def sum_at_owner(x, axis, dim):
    size = lax.axis_size(axis)
    blocks = lax.all_to_all(cut_along(x, dim, size), axis, 0, 0, tiled=True)
    return jnp.sum(blocks.astype(jnp.float32), axis=0)


def taken_together(x, axis):
    everything = copy_for_each(x, axis)
    return jnp.sum(everything.astype(jnp.float32), axis=0)


def rows_first(arrays, axis, dims):
    turned = [jnp.moveaxis(a, dim, 0) for a, dim in zip(arrays, dims)]
    both = jnp.concatenate([t.reshape(len(t), -1) for t in turned], axis=1)
    filled, at, outs = (lax.all_gather(both, axis, axis=0, tiled=True), 0, [])
    for t, dim in zip(turned, dims):
        share = filled[:, at : at + t[0].size].reshape(-1, *t.shape[1:])
        outs.append(jnp.moveaxis(share, 0, dim))
        at += t[0].size
    return tuple(outs)


def collected_together(x, axis):
    leaves = jax.tree.leaves(x)
    turns = sorted(range(len(leaves)), key=lambda k: -leaves[k].size)
    width = (1, *leaves[turns[0]].shape)[-1]
    lines = [
        jnp.pad(leaves[k].reshape(-1), (0, -leaves[k].size % width)).reshape(-1, width)
        for k in turns
    ]
    both, at, found = (lax.all_gather(jnp.concatenate(lines), axis), 0, {})
    for k, line in zip(turns, lines):
        share = both[:, at : at + len(line)].reshape(len(both), -1)
        found[k] = share[:, : leaves[k].size].reshape(-1, *leaves[k].shape)
        at += len(line)
    numbers = iter(range(len(leaves)))
    return jax.tree.map(lambda _: found[next(numbers)], x)


def joined_all(x, axes, combine):
    for axis in axes:
        pieces = collected_together(x, axis)
        x = jax.tree.map(lambda part: part[0], pieces)
        for k in range(1, lax.axis_size(axis)):
            x = combine(x, jax.tree.map(lambda part: part[k], pieces))
    return x


def rms_scale(values, gain):
    mean_sq = jnp.mean(values * values, axis=-1, keepdims=True)
    return values * lax.rsqrt(mean_sq + norm_eps) * gain


def route_gates(normed, router, chosen, n_experts):
    logits = jnp.dot(normed, router, preferred_element_type=jnp.float32)
    marks = (chosen[:, :, None] == jnp.arange(n_experts, dtype=jnp.int32)[None, None, :]).astype(
        jnp.float32
    )
    picked = jnp.sum(logits[:, None, :] * marks, axis=2)
    first = 1.0 / (1.0 + jnp.exp(picked[:, 1] - picked[:, 0]))
    second = 1.0 / (1.0 + jnp.exp(picked[:, 0] - picked[:, 1]))
    return jnp.stack([first, second], axis=1)


def slot_tables(block_routes, block_gates, expert, capacity, n_experts):
    flat = block_routes.reshape(-1)
    marks = (flat[:, None] == jnp.arange(n_experts, dtype=jnp.int32)[None, :]).astype(jnp.int32)
    earlier = jnp.cumsum(marks, axis=0) - marks
    rank = jnp.sum(earlier * marks, axis=1).reshape(block_routes.shape)
    mine = block_routes == expert
    hits = (
        mine[:, :, None]
        & (rank[:, :, None] == jnp.arange(capacity, dtype=jnp.int32)[None, None, :])
    ).astype(jnp.float32)
    select = jnp.transpose(jnp.sum(hits, axis=1))
    combine = jnp.sum(hits * block_gates[:, :, None], axis=1)
    return (select, combine)


def swiglu(rows, gate_mat, up_mat):
    gate_part = jnp.dot(rows, gate_mat, preferred_element_type=jnp.float32)
    up_part = jnp.dot(rows, up_mat, preferred_element_type=jnp.float32)
    return (jax.nn.silu(gate_part) * up_part).astype(jnp.bfloat16)


def steer_attention(steer_query, steer_cache, steer_new, cache_len):
    models, seq_rows, width = steer_query.shape
    heads = width // HEAD_DIM
    span = steer_cache.shape[3]
    scale = 1.0 / math.sqrt(HEAD_DIM)
    queries = steer_query.reshape(models, seq_rows, heads, HEAD_DIM)
    keys = steer_cache[:, 0].reshape(models, seq_rows, span, heads, HEAD_DIM)
    values = steer_cache[:, 1].reshape(models, seq_rows, span, heads, HEAD_DIM)
    new_keys = steer_new[:, 0].reshape(models, seq_rows, heads, HEAD_DIM)
    new_values = steer_new[:, 1].reshape(models, seq_rows, heads, HEAD_DIM).astype(jnp.float32)
    scores = (
        jnp.einsum("mshd,msphd->mshp", queries, keys, preferred_element_type=jnp.float32) * scale
    )
    new_score = (
        jnp.einsum("mshd,mshd->msh", queries, new_keys, preferred_element_type=jnp.float32) * scale
    )
    live = (jnp.arange(span, dtype=jnp.int32)[None, :] < cache_len[:, None])[None, :, None, :]
    masked = jnp.where(live, scores, -1e30)
    summit = jnp.maximum(jnp.max(masked, axis=3), new_score)
    expo = jnp.where(live, jnp.exp(masked - summit[..., None]), 0.0)
    new_expo = jnp.exp(new_score - summit)
    denom = jnp.sum(expo, axis=3) + new_expo
    weights = (expo / denom[..., None]).astype(jnp.bfloat16)
    new_weight = (new_expo / denom).astype(jnp.bfloat16).astype(jnp.float32)
    attended = jnp.einsum("mshp,msphd->mshd", weights, values, preferred_element_type=jnp.float32)
    attended = attended + new_weight[..., None] * new_values
    return attended.reshape(models, seq_rows, width).astype(jnp.bfloat16)


def merge_pair(first, second):
    summit = jnp.maximum(first[0], second[0])
    return (summit, first[1] * jnp.exp(first[0] - summit) + second[1] * jnp.exp(second[0] - summit))


def per_device(
    tokens,
    norm_gain,
    router,
    w_gate,
    w_up,
    w_down,
    final_gain,
    routes,
    steer_hidden,
    steer_query,
    steer_cache,
    steer_new,
    cache_len,
    steer_out,
    steer_gain,
    base_head,
    steer_head,
    inv_temp,
):
    n_experts = lax.axis_size(MP)
    expert = lax.axis_index(MP)
    seq_rows = tokens.shape[0]
    capacity = 4 * seq_rows // n_experts
    gate_mat = w_gate[0]
    up_mat = w_up[0]
    down_mat = w_down[0]
    attended = steer_attention(steer_query, steer_cache, steer_new, cache_len)
    proj = jnp.einsum("msw,mwv->msv", attended, steer_out, preferred_element_type=jnp.float32)
    proj = over_copies(proj, MP)
    steer_state = steer_hidden.astype(jnp.float32) + proj
    steer_normed = rms_scale(steer_state, steer_gain[:, None, :]).astype(jnp.bfloat16)
    resid = tokens.astype(jnp.float32)
    normed = rms_scale(resid, norm_gain).astype(jnp.bfloat16)
    first_row = lax.axis_index(DP) * seq_rows
    own_routes = lax.dynamic_slice_in_dim(routes, first_row, seq_rows, 0)
    gates = route_gates(normed, router, own_routes, n_experts)
    select, combine = slot_tables(own_routes, gates, expert, capacity, n_experts)
    slot_in = jnp.dot(
        select.astype(jnp.bfloat16), normed, preferred_element_type=jnp.float32
    ).astype(jnp.bfloat16)
    hidden = swiglu(gathered_copies(slot_in, DP, 0), gate_mat, up_mat)
    slot_out = sum_at_owner(
        jnp.dot(hidden, down_mat, preferred_element_type=jnp.float32).astype(jnp.bfloat16), DP, 0
    )
    mixed = jnp.dot(combine, slot_out, precision=lax.Precision.HIGHEST)
    moe = taken_together(mixed.astype(jnp.bfloat16), MP).astype(jnp.float32)
    base_normed = rms_scale(resid + moe, final_gain).astype(jnp.bfloat16)
    base_all, steer_all = rows_first((base_normed[None], steer_normed), DP, (1, 1))
    base_all = base_all[0]
    base_logits = jnp.dot(base_all, base_head, preferred_element_type=jnp.float32)
    plus = jnp.dot(steer_all[0], steer_head[0], preferred_element_type=jnp.float32)
    minus = jnp.dot(steer_all[1], steer_head[1], preferred_element_type=jnp.float32)
    combined = inv_temp[:, None] * (base_logits + steer_alpha * (plus - minus))
    local_peak = jnp.max(combined, axis=1)
    local_total = jnp.sum(jnp.exp(combined - local_peak[:, None]), axis=1)
    peak_val, total = joined_all((local_peak, local_total), DP_MP, merge_pair)
    return combined - peak_val[:, None] - jnp.log(total)[:, None]


def solution(mesh):
    finer = Mesh(mesh.devices.reshape(4, 4, 4, 2), ("dp_0", "dp_1", "mp_0", "mp_1"))
    placed = (
        P(DP, None),
        P(),
        P(),
        P(MP, None, DP),
        P(MP, None, DP),
        P(MP, DP, None),
        P(),
        P(),
        P(None, DP, None),
        P(None, DP, MP),
        P(None, None, DP, None, MP),
        P(None, None, DP, MP),
        P(DP),
        P(None, MP, None),
        P(),
        P(None, DP_MP),
        P(None, None, DP_MP),
        P(),
    )
    return jax.shard_map(
        per_device, mesh=finer, in_specs=placed, out_specs=P(None, DP_MP), check_vma=False
    )
```

profile of v0, /device:TPU:1, one launch (start us, length us, event | category | flops | bytes accessed | tf_op | source)
XLA Modules:
  0.0 206.8 jit_solution(15885888711797221466)
XLA Ops:
  6.5 1.1 fusion.41
  7.7 0.8 broadcast_compare_fusion
  8.5 1.1 fusion.49
  9.7 0.1 eq.51
  9.9 0.2 select_reduce_fusion
  10.2 0.1 copy.57
  10.3 1.1 convolution_convert_fusion.1
  11.5 1.1 broadcast_in_dim.24
  12.6 8.4 %all-to-all-start = ((bf16[16,8,4096]{2,1,0:T(8,128)(2,1)}), bf16[16,8,4096]{2,1,0:T(8,128)(2,1)S(1)}, u32[]{:S(2)}, u32[]{:S(2)}) async-start(bf16[16,8,4096]{2,1,0:T(8,128)(2,1)} %broadcast_in_dim.24), calls=%async_computation | async-start | bytes 2097152 | tf_op jit(solution)/shard_map/all_to_all | solution.py:18
  21.0 0.8 fusion.53
  21.8 0.7 iota_compare_fusion.1
  22.5 1.4 fusion.32
  24.0 13.0 %all-to-all-done = bf16[16,8,4096]{2,1,0:T(8,128)(2,1)S(1)} async-done(((bf16[16,8,4096]{2,1,0:T(8,128)(2,1)}), bf16[16,8,4096]{2,1,0:T(8,128)(2,1)S(1)}, u32[]{:S(2)}, u32[]{:S(2)}) %all-to-all-start) | async-done | bytes 1048608 | tf_op jit(solution)/shard_map/all_to_all | solution.py:18
  37.0 4.3 %fusion.4 = f32[128,896]{1,0:T(8,128)S(1)} fusion(bf16[1,4096,896]{2,1,0:T(8,128)(2,1)} %param.21, bf16[16,8,4096]{2,1,0:T(8,128)(2,1)S(1)} %all-to-all-done), kind=kOutput, calls=%fused_computation.4 | convolution fusion | flops 939524096 | bytes 8847360 | tf_op jit(solution)/shard_map/dot_general | solution.py:122
  41.4 8.6 %fusion.9 = bf16[16,8,4096]{2,1,0:T(8,128)(2,1)} fusion(bf16[1,896,4096]{2,1,0:T(8,128)(2,1)} %param.23, bf16[1,4096,896]{2,1,0:T(8,128)(2,1)} %param.22, bf16[16,8,4096]{2,1,0:T(8,128)(2,1)S(1)} %all-to-all-done, f32[128,896]{1,0:T(8,128)S(1)} %fusion.4), kind=kOutput, calls=%fused_computation.7 | convolution fusion | flops 1880260608 | bytes 17235968 | tf_op jit(solution)/shard_map/dot_general | solution.py:204
  50.1 4.3 %all-to-all-start.1 = ((bf16[16,8,4096]{2,1,0:T(8,128)(2,1)}), bf16[16,8,4096]{2,1,0:T(8,128)(2,1)S(1)}, u32[]{:S(2)}, u32[]{:S(2)}) async-start(bf16[16,8,4096]{2,1,0:T(8,128)(2,1)} %fusion.9), calls=%async_computation.1 | async-start | bytes 2097152 | tf_op jit(solution)/shard_map/all_to_all | solution.py:44
  54.4 0.2 fusion.58
  54.6 0.1 fusion.64
  54.7 1.3 fusion.30
  56.0 0.2 fusion.59
  56.2 13.3 %all-to-all-done.1 = bf16[16,8,4096]{2,1,0:T(8,128)(2,1)S(1)} async-done(((bf16[16,8,4096]{2,1,0:T(8,128)(2,1)}), bf16[16,8,4096]{2,1,0:T(8,128)(2,1)S(1)}, u32[]{:S(2)}, u32[]{:S(2)}) %all-to-all-start.1) | async-done | bytes 1048608 | tf_op jit(solution)/shard_map/all_to_all | solution.py:44
  69.6 1.1 broadcast_in_dim.29
  70.7 7.7 %all-to-all-start.3 = ((f32[8,2,16,1024]{3,2,1,0:T(8,128)}), f32[8,2,16,1024]{3,2,1,0:T(8,128)S(1)}, u32[]{:S(2)}, u32[]{:S(2)}) async-start(f32[8,2,16,1024]{3,2,1,0:T(8,128)} %broadcast_in_dim.29), calls=%async_computation.3 | async-start | bytes 2097152 | tf_op jit(solution)/shard_map/all_to_all | solution.py:18
  78.3 0.1 convert_reduce_fusion.1
  78.5 0.4 convolution_convert_fusion
  78.9 14.4 %all-to-all-done.3 = f32[8,2,16,1024]{3,2,1,0:T(8,128)S(1)} async-done(((f32[8,2,16,1024]{3,2,1,0:T(8,128)}), f32[8,2,16,1024]{3,2,1,0:T(8,128)S(1)}, u32[]{:S(2)}, u32[]{:S(2)}) %all-to-all-start.3) | async-done | bytes 1048608 | tf_op jit(solution)/shard_map/all_to_all | solution.py:18
  93.3 1.1 broadcast_in_dim.25
  94.4 4.4 %all-to-all-start.2 = ((bf16[8,16,4096]{2,1,0:T(8,128)(2,1)}), bf16[8,16,4096]{2,1,0:T(8,128)(2,1)S(1)}, u32[]{:S(2)}, u32[]{:S(2)}) async-start(bf16[8,16,4096]{2,1,0:T(8,128)(2,1)} %broadcast_in_dim.25), calls=%async_computation.2 | async-start | bytes 2097152 | tf_op jit(solution)/shard_map/all_to_all | solution.py:18
  98.9 0.1 multiply_reduce_fusion.1
  99.1 14.7 %all-to-all-done.2 = bf16[8,16,4096]{2,1,0:T(8,128)(2,1)S(1)} async-done(((bf16[8,16,4096]{2,1,0:T(8,128)(2,1)}), bf16[8,16,4096]{2,1,0:T(8,128)(2,1)S(1)}, u32[]{:S(2)}, u32[]{:S(2)}) %all-to-all-start.2) | async-done | bytes 1048608 | tf_op jit(solution)/shard_map/all_to_all | solution.py:18
  113.8 0.1 convert_reduce_fusion
  114.0 0.2 multiply_reduce_fusion
  114.1 0.1 multiply_convert_fusion
  114.2 0.7 pad_maximum_fusion
  115.0 2.1 %fusion.109 = (bf16[1,1024,125]{1,0,2:T(2,128)(2,1)S(1)}, bf16[1,1024,125]{1,0,2:T(2,128)(2,1)S(1)}) fusion(bf16[2,1024,125]{1,0,2:T(2,128)(2,1)} %param.34), kind=kLoop, calls=%fused_computation.162 | loop fusion | bytes 1024000 | tf_op jit(solution)/shard_map/slice | solution.py:213
  117.1 0.5 copy.75
  117.5 1.1 copy.74
  118.6 39.7 %all-gather.10.cloned.1.call-done = bf16[256,6144]{1,0:T(8,128)(2,1)} async-done(((bf16[16,6144]{1,0:T(8,128)(2,1)}), bf16[256,6144]{1,0:T(8,128)(2,1)}) %all-gather.10.cloned.1.call-update) | async-done | bytes 3145744 | tf_op jit(solution)/shard_map/all_gather | solution.py:56
  158.4 1.3 slice.227
  159.6 0.5 copy.73
  160.2 1.2 fusion.29
  161.4 2.4 %fusion.12 = f32[256,125]{0,1:T(8,128)S(1)} fusion(bf16[4096,125]{1,0:T(8,128)(2,1)S(1)} %copy-done, bf16[256,6144]{1,0:T(8,128)(2,1)} %all-gather.10.cloned.1.call-done), kind=kOutput, calls=%fused_computation.10 | convolution fusion | flops 262144000 | bytes 3249152 | tf_op jit(solution)/shard_map/dot_general | solution.py:211
  163.8 0.3 fusion.111
  164.2 8.1 %all-gather.4 = f32[4,2,256]{2,1,0:T(2,128)S(1)} all-gather(f32[1,2,256]{2,1,0:T(2,128)S(1)} %maximum_bitcast_fusion), channel_id=2, replica_groups=mesh['dp_0'=4,'dp_1'=4,'mp_0'=4,'mp_1'=2] {'dp_0'}, dimensions={0}, use_global_device_ids=true | all-gather | bytes 10240 | tf_op jit(solution)/shard_map/all_gather | solution.py:72
  172.4 8.1 %all-gather.5 = f32[4,2,256]{2,1,0:T(2,128)S(1)} all-gather(f32[1,2,256]{2,1,0:T(2,128)S(1)} %maximum_bitcast_fusion.1), channel_id=3, replica_groups=mesh['dp_0'=4,'dp_1'=4,'mp_0'=4,'mp_1'=2] {'dp_1'}, dimensions={0}, use_global_device_ids=true | all-gather | bytes 10240 | tf_op jit(solution)/shard_map/all_gather | solution.py:72
  180.6 8.5 %all-gather.6 = f32[4,2,256]{2,1,0:T(2,128)S(1)} all-gather(f32[1,2,256]{2,1,0:T(2,128)S(1)} %maximum_bitcast_fusion.2), channel_id=4, replica_groups=mesh['dp_0'=4,'dp_1'=4,'mp_0'=4,'mp_1'=2] {'mp_0'}, dimensions={0}, use_global_device_ids=true | all-gather | bytes 10240 | tf_op jit(solution)/shard_map/all_gather | solution.py:72
  189.1 10.1 %all-gather.7 = f32[2,2,256]{2,1,0:T(2,128)S(1)} all-gather(f32[1,2,256]{2,1,0:T(2,128)S(1)} %maximum_bitcast_fusion.3), channel_id=5, replica_groups=mesh['dp_0'=4,'dp_1'=4,'mp_0'=4,'mp_1'=2] {'mp_1'}, dimensions={0}, use_global_device_ids=true | all-gather | bytes 6144 | tf_op jit(solution)/shard_map/all_gather | solution.py:72
  199.2 0.8 copy.64
  (46 shorter events, 0.9 us)
Async XLA Ops:
  6.5 154.9 %copy-start = (bf16[4096,125]{1,0:T(8,128)(2,1)S(1)}, bf16[4096,125]{1,0:T(8,128)(2,1)}, u32[]{:S(2)}) copy-start(bf16[4096,125]{1,0:T(8,128)(2,1)} %param.33) | copy-start | bytes 3072004
  12.6 24.5 %all-to-all-start = ((bf16[16,8,4096]{2,1,0:T(8,128)(2,1)}), bf16[16,8,4096]{2,1,0:T(8,128)(2,1)S(1)}, u32[]{:S(2)}, u32[]{:S(2)}) async-start(bf16[16,8,4096]{2,1,0:T(8,128)(2,1)} %broadcast_in_dim.24), calls=%async_computation | async-start | bytes 2097152 | tf_op jit(solution)/shard_map/all_to_all | solution.py:18
  41.4 14.6 %copy-start.2 = (bf16[2,128,1024]{2,1,0:T(8,128)(2,1)S(1)}, bf16[2,128,1024]{2,1,0:T(8,128)(2,1)}, u32[]{:S(2)}) copy-start(bf16[2,128,1024]{2,1,0:T(8,128)(2,1)} %param.31) | copy-start | bytes 1572868
  41.4 14.6 %copy-start.4 = (bf16[2,2,16,128]{3,2,1,0:T(8,128)(2,1)S(1)}, bf16[2,2,16,128]{3,2,1,0:T(8,128)(2,1)}, u32[]{:S(2)}) copy-start(bf16[2,2,16,128]{3,2,1,0:T(8,128)(2,1)} %param.29) | copy-start | bytes 49156
  50.0 48.8 %copy-start.3 = (bf16[2,16,1024]{2,1,0:T(8,128)(2,1)S(1)}, bf16[2,16,1024]{2,1,0:T(8,128)(2,1)}, u32[]{:S(2)}) copy-start(bf16[2,16,1024]{2,1,0:T(8,128)(2,1)} %param.26) | copy-start | bytes 196612
  50.0 49.0 %copy-start.6 = (f32[2,1024]{1,0:T(2,128)S(1)}, f32[2,1024]{1,0:T(2,128)}, u32[]{:S(2)}) copy-start(f32[2,1024]{1,0:T(2,128)} %param.32) | copy-start | bytes 24580
  50.0 63.9 %copy-start.1 = (bf16[16,4096]{1,0:T(8,128)(2,1)S(1)}, bf16[16,4096]{1,0:T(8,128)(2,1)}, u32[]{:S(2)}) copy-start(bf16[16,4096]{1,0:T(8,128)(2,1)} %param.18) | copy-start | bytes 393220
  50.0 64.1 %copy-start.5 = (f32[4096]{0:T(1024)S(1)}, f32[4096]{0:T(1024)}, u32[]{:S(2)}) copy-start(f32[4096]{0:T(1024)} %param.24) | copy-start | bytes 49156
  50.1 19.5 %all-to-all-start.1 = ((bf16[16,8,4096]{2,1,0:T(8,128)(2,1)}), bf16[16,8,4096]{2,1,0:T(8,128)(2,1)S(1)}, u32[]{:S(2)}, u32[]{:S(2)}) async-start(bf16[16,8,4096]{2,1,0:T(8,128)(2,1)} %fusion.9), calls=%async_computation.1 | async-start | bytes 2097152 | tf_op jit(solution)/shard_map/all_to_all | solution.py:44
  70.7 22.6 %all-to-all-start.3 = ((f32[8,2,16,1024]{3,2,1,0:T(8,128)}), f32[8,2,16,1024]{3,2,1,0:T(8,128)S(1)}, u32[]{:S(2)}, u32[]{:S(2)}) async-start(f32[8,2,16,1024]{3,2,1,0:T(8,128)} %broadcast_in_dim.29), calls=%async_computation.3 | async-start | bytes 2097152 | tf_op jit(solution)/shard_map/all_to_all | solution.py:18
  94.4 19.4 %all-to-all-start.2 = ((bf16[8,16,4096]{2,1,0:T(8,128)(2,1)}), bf16[8,16,4096]{2,1,0:T(8,128)(2,1)S(1)}, u32[]{:S(2)}, u32[]{:S(2)}) async-start(bf16[8,16,4096]{2,1,0:T(8,128)(2,1)} %broadcast_in_dim.25), calls=%async_computation.2 | async-start | bytes 2097152 | tf_op jit(solution)/shard_map/all_to_all | solution.py:18
  98.8 59.5 %all-gather.10.cloned.1.call-start = ((), (), s32[]{:S(2)}) async-start(), calls=%async_computation.4 | async-start | bytes 3342336 | tf_op jit(solution)/shard_map/all_gather | solution.py:56
  99.1 64.7 %copy-start.7 = (f32[256]{0:T(256)S(1)}, f32[256]{0:T(256)}, u32[]{:S(2)}) copy-start(f32[256]{0:T(256)} %param.35) | copy-start | bytes 3076
Sparse Core Ops, SparseCore 0:
  115.1 43.2 all-gather.9
where the time goes:
time: 208 us; the launch traced here: 207 us
  waiting for transfers between devices  95.2 us (46%)
  blocking collectives  34.8 us (17%)
  starting transfers between devices  24.8 us (12%)
  matrix products  22.5 us (11%)
  between operations  13.7 us (7%)
  local copies, waits for them, and re-layouts  9.92 us (5%)
  other arithmetic  5.86 us (3%)
    all_to_all x3, waiting for transfers between devices, copy_for_each(): lax.all_to_all(jnp.broadcast_to(x[None], (size, *x.shape)), axis, 0, 0, t...  42.1 us
    all_gather x1, waiting for transfers between devices, rows_first(): filled, at, outs = (lax.all_gather(both, axis, axis=0, tiled=True), 0, [])  39.7 us
    all_gather x4, blocking collectives, collected_together(): both, at, found = (lax.all_gather(jnp.concatenate(lines), axis), 0, {})  34.8 us
    all_to_all x3, starting transfers between devices, copy_for_each(): lax.all_to_all(jnp.broadcast_to(x[None], (size, *x.shape)), axis, 0, 0, t...  20.5 us
    all_to_all x1, waiting for transfers between devices, sum_at_owner(): blocks = lax.all_to_all(cut_along(x, dim, size), axis, 0, 0, tiled=True)  13.3 us
    dot_general x1, matrix products, per_device(): jnp.dot(hidden, down_mat, preferred_element_type=jnp.float32)  8.64 us
    all_to_all x1, starting transfers between devices, sum_at_owner(): blocks = lax.all_to_all(cut_along(x, dim, size), axis, 0, 0, tiled=True)  4.35 us
    dot_general x1, matrix products, swiglu(): gate_part = jnp.dot(rows, gate_mat, preferred_element_type=jnp.float32)  4.34 us
  transfers between devices with their start and end apart: 5, of which 5 were waited for; matrix products, arithmetic and copies ran while one was open for 5% of the time, Pallas kernels for 0%

commit v1 on v0

--- a/solution.py
+++ b/solution.py
@@ -53,7 +53,14 @@
 def rows_first(arrays, axis, dims):
     turned = [jnp.moveaxis(a, dim, 0) for a, dim in zip(arrays, dims)]
     both = jnp.concatenate([t.reshape(len(t), -1) for t in turned], axis=1)
-    filled, at, outs = (lax.all_gather(both, axis, axis=0, tiled=True), 0, [])
+
+    def follow_slabs(z, named_axis, dimension_no):
+        inter = tuple((z for _ in range(lax.psum(1, axis_name=named_axis))))
+        main = jnp.stack(inter, axis=0)
+        res = lax.all_to_all(main, concat_axis=0, split_axis=0, axis_name=named_axis)
+        return jnp.concatenate(res, axis=dimension_no)
+
+    filled, at, outs = (follow_slabs(both, axis, 0), 0, [])
     for t, dim in zip(turned, dims):
         share = filled[:, at : at + t[0].size].reshape(-1, *t.shape[1:])
         outs.append(jnp.moveaxis(share, 0, dim))

time: 208 us -> 203 us (0.976)
  between operations: 13.7 us -> 0.31 us
  waiting for transfers between devices: 95.2 us -> 99.9 us
  starting transfers between devices: 24.8 us -> 29.3 us
    all_to_all x0 -> x1, waiting for transfers between devices: none -> 44.5 us  [follow_slabs(): lax.all_to_all(main, concat_axis=0, split_axis=0, axis_name=named_axis)]
    all_gather x1 -> x0, waiting for transfers between devices: 39.7 us -> none  [rows_first(): filled, at, outs = (lax.all_gather(both, axis, axis=0, tiled=True), 0, [])]
    all_to_all x0 -> x1, starting transfers between devices: none -> 4.48 us  [follow_slabs(): lax.all_to_all(main, concat_axis=0, split_axis=0, axis_name=named_axis)]
  transfers between devices with their start and end apart: 5 -> 5, of which waited for: 5 -> 5; matrix products, arithmetic and copies ran while one was open for 5% -> 4% of each run, Pallas kernels for 0% -> 0%
where the time goes in v1:
time: 203 us; the launch traced here: 202 us
  waiting for transfers between devices  99.9 us (49%)
  blocking collectives  34.6 us (17%)
  starting transfers between devices  29.3 us (14%)
  matrix products  22.5 us (11%)
  local copies, waits for them, and re-layouts  10.6 us (5%)
  other arithmetic  5.16 us (3%)
    all_to_all x1, waiting for transfers between devices, follow_slabs(): lax.all_to_all(main, concat_axis=0, split_axis=0, axis_name=named_axis)  44.5 us
    all_to_all x3, waiting for transfers between devices, copy_for_each(): lax.all_to_all(jnp.broadcast_to(x[None], (size, *x.shape)), axis, 0, 0, t...  42.1 us
    all_gather x4, blocking collectives, collected_together(): both, at, found = (lax.all_gather(jnp.concatenate(lines), axis), 0, {})  34.6 us
    all_to_all x3, starting transfers between devices, copy_for_each(): lax.all_to_all(jnp.broadcast_to(x[None], (size, *x.shape)), axis, 0, 0, t...  20.5 us
    all_to_all x1, waiting for transfers between devices, sum_at_owner(): blocks = lax.all_to_all(cut_along(x, dim, size), axis, 0, 0, tiled=True)  13.3 us
    dot_general x1, matrix products, per_device(): jnp.dot(hidden, down_mat, preferred_element_type=jnp.float32)  8.64 us
    all_to_all x1, starting transfers between devices, follow_slabs(): lax.all_to_all(main, concat_axis=0, split_axis=0, axis_name=named_axis)  4.48 us
    all_to_all x1, starting transfers between devices, sum_at_owner(): blocks = lax.all_to_all(cut_along(x, dim, size), axis, 0, 0, tiled=True)  4.34 us
  transfers between devices with their start and end apart: 5, of which 5 were waited for; matrix products, arithmetic and copies ran while one was open for 4% of the time, Pallas kernels for 0%

profile of v1, /device:TPU:1, one launch (start us, length us, event | category | flops | bytes accessed | tf_op | source)
XLA Modules:
  0.0 202.4 jit_solution(16520374781583903837)
XLA Ops:
  0.0 1.1 fusion.41
  1.2 0.8 broadcast_compare_fusion
  2.0 1.1 fusion.49
  3.2 0.1 eq.51
  3.4 0.2 select_reduce_fusion
  3.8 1.1 convolution_convert_fusion.1
  4.9 1.1 broadcast_in_dim.24
  6.0 8.4 %all-to-all-start = ((bf16[16,8,4096]{2,1,0:T(8,128)(2,1)}), bf16[16,8,4096]{2,1,0:T(8,128)(2,1)S(1)}, u32[]{:S(2)}, u32[]{:S(2)}) async-start(bf16[16,8,4096]{2,1,0:T(8,128)(2,1)} %broadcast_in_dim.24), calls=%async_computation | async-start | bytes 2097152 | tf_op jit(solution)/shard_map/all_to_all | solution.py:18
  14.4 0.8 fusion.53
  15.3 0.7 iota_compare_fusion.1
  16.0 1.4 fusion.32
  17.5 13.0 %all-to-all-done = bf16[16,8,4096]{2,1,0:T(8,128)(2,1)S(1)} async-done(((bf16[16,8,4096]{2,1,0:T(8,128)(2,1)}), bf16[16,8,4096]{2,1,0:T(8,128)(2,1)S(1)}, u32[]{:S(2)}, u32[]{:S(2)}) %all-to-all-start) | async-done | bytes 1048608 | tf_op jit(solution)/shard_map/all_to_all | solution.py:18
  30.5 4.3 %fusion.4 = f32[128,896]{1,0:T(8,128)S(1)} fusion(bf16[1,4096,896]{2,1,0:T(8,128)(2,1)} %param.21, bf16[16,8,4096]{2,1,0:T(8,128)(2,1)S(1)} %all-to-all-done), kind=kOutput, calls=%fused_computation.4 | convolution fusion | flops 939524096 | bytes 8847360 | tf_op jit(solution)/shard_map/dot_general | solution.py:129
  34.9 8.6 %fusion.9 = bf16[16,8,4096]{2,1,0:T(8,128)(2,1)} fusion(bf16[1,896,4096]{2,1,0:T(8,128)(2,1)} %param.23, bf16[1,4096,896]{2,1,0:T(8,128)(2,1)} %param.22, bf16[16,8,4096]{2,1,0:T(8,128)(2,1)S(1)} %all-to-all-done, f32[128,896]{1,0:T(8,128)S(1)} %fusion.4), kind=kOutput, calls=%fused_computation.7 | convolution fusion | flops 1880260608 | bytes 17235968 | tf_op jit(solution)/shard_map/dot_general | solution.py:211
  43.5 4.3 %all-to-all-start.1 = ((bf16[16,8,4096]{2,1,0:T(8,128)(2,1)}), bf16[16,8,4096]{2,1,0:T(8,128)(2,1)S(1)}, u32[]{:S(2)}, u32[]{:S(2)}) async-start(bf16[16,8,4096]{2,1,0:T(8,128)(2,1)} %fusion.9), calls=%async_computation.1 | async-start | bytes 2097152 | tf_op jit(solution)/shard_map/all_to_all | solution.py:44
  47.9 0.2 fusion.58
  48.0 0.1 fusion.64
  48.1 1.3 fusion.30
  49.4 0.2 fusion.59
  49.7 13.3 %all-to-all-done.1 = bf16[16,8,4096]{2,1,0:T(8,128)(2,1)S(1)} async-done(((bf16[16,8,4096]{2,1,0:T(8,128)(2,1)}), bf16[16,8,4096]{2,1,0:T(8,128)(2,1)S(1)}, u32[]{:S(2)}, u32[]{:S(2)}) %all-to-all-start.1) | async-done | bytes 1048608 | tf_op jit(solution)/shard_map/all_to_all | solution.py:44
  63.0 1.1 broadcast_in_dim.29
  64.1 7.7 %all-to-all-start.3 = ((f32[8,2,16,1024]{3,2,1,0:T(8,128)}), f32[8,2,16,1024]{3,2,1,0:T(8,128)S(1)}, u32[]{:S(2)}, u32[]{:S(2)}) async-start(f32[8,2,16,1024]{3,2,1,0:T(8,128)} %broadcast_in_dim.29), calls=%async_computation.3 | async-start | bytes 2097152 | tf_op jit(solution)/shard_map/all_to_all | solution.py:18
  71.8 0.1 convert_reduce_fusion.1
  71.9 0.4 convolution_convert_fusion
  72.4 14.4 %all-to-all-done.3 = f32[8,2,16,1024]{3,2,1,0:T(8,128)S(1)} async-done(((f32[8,2,16,1024]{3,2,1,0:T(8,128)}), f32[8,2,16,1024]{3,2,1,0:T(8,128)S(1)}, u32[]{:S(2)}, u32[]{:S(2)}) %all-to-all-start.3) | async-done | bytes 1048608 | tf_op jit(solution)/shard_map/all_to_all | solution.py:18
  86.8 1.1 broadcast_in_dim.25
  87.9 4.4 %all-to-all-start.2 = ((bf16[8,16,4096]{2,1,0:T(8,128)(2,1)}), bf16[8,16,4096]{2,1,0:T(8,128)(2,1)S(1)}, u32[]{:S(2)}, u32[]{:S(2)}) async-start(bf16[8,16,4096]{2,1,0:T(8,128)(2,1)} %broadcast_in_dim.25), calls=%async_computation.2 | async-start | bytes 2097152 | tf_op jit(solution)/shard_map/all_to_all | solution.py:18
  92.4 0.1 multiply_reduce_fusion.1
  92.6 14.7 %all-to-all-done.2 = bf16[8,16,4096]{2,1,0:T(8,128)(2,1)S(1)} async-done(((bf16[8,16,4096]{2,1,0:T(8,128)(2,1)}), bf16[8,16,4096]{2,1,0:T(8,128)(2,1)S(1)}, u32[]{:S(2)}, u32[]{:S(2)}) %all-to-all-start.2) | async-done | bytes 1048608 | tf_op jit(solution)/shard_map/all_to_all | solution.py:18
  107.3 0.1 convert_reduce_fusion
  107.4 0.2 multiply_reduce_fusion
  107.6 0.1 multiply_convert_fusion
  107.7 2.1 %stack.5 = bf16[16,16,6144]{2,1,0:T(8,128)(2,1)} broadcast(bf16[16,6144]{1,0:T(8,128)(2,1)S(1)} %pad_maximum_fusion), dimensions={1,2} | broadcast | bytes 3342336 | tf_op jit(solution)/shard_map/stack | solution.py:59
  109.8 4.5 %all-to-all-start.4 = ((bf16[16,16,6144]{2,1,0:T(8,128)(2,1)}), bf16[16,16,6144]{2,1,0:T(8,128)(2,1)}, u32[]{:S(2)}, u32[]{:S(2)}) async-start(bf16[16,16,6144]{2,1,0:T(8,128)(2,1)} %stack.5), calls=%async_computation.4 | async-start | bytes 6291456 | tf_op jit(solution)/shard_map/all_to_all | solution.py:60
  114.3 0.7 fusion.109
  115.0 1.1 copy.83
  116.1 0.5 copy.84
  116.6 44.5 %all-to-all-done.4 = bf16[16,16,6144]{2,1,0:T(8,128)(2,1)} async-done(((bf16[16,16,6144]{2,1,0:T(8,128)(2,1)}), bf16[16,16,6144]{2,1,0:T(8,128)(2,1)}, u32[]{:S(2)}, u32[]{:S(2)}) %all-to-all-start.4) | async-done | bytes 3145760 | tf_op jit(solution)/shard_map/all_to_all | solution.py:60
  161.1 1.3 slice.227
  162.4 0.5 copy.69
  162.9 2.4 %fusion.12 = f32[256,125]{0,1:T(8,128)S(1)} fusion(bf16[4096,125]{1,0:T(8,128)(2,1)S(1)} %copy-done, bf16[256,6144]{1,0:T(8,128)(2,1)} %bitcast.16), kind=kOutput, calls=%fused_computation.10 | convolution fusion | flops 262144000 | bytes 3249152 | tf_op jit(solution)/shard_map/dot_general | solution.py:218
  165.3 1.2 fusion.29
  166.6 0.3 fusion.111
  166.9 8.1 %all-gather.4 = f32[4,2,256]{2,1,0:T(2,128)S(1)} all-gather(f32[1,2,256]{2,1,0:T(2,128)S(1)} %maximum_bitcast_fusion), channel_id=2, replica_groups=mesh['dp_0'=4,'dp_1'=4,'mp_0'=4,'mp_1'=2] {'dp_0'}, dimensions={0}, use_global_device_ids=true | all-gather | bytes 10240 | tf_op jit(solution)/shard_map/all_gather | solution.py:79
  175.1 8.1 %all-gather.5 = f32[4,2,256]{2,1,0:T(2,128)S(1)} all-gather(f32[1,2,256]{2,1,0:T(2,128)S(1)} %maximum_bitcast_fusion.1), channel_id=3, replica_groups=mesh['dp_0'=4,'dp_1'=4,'mp_0'=4,'mp_1'=2] {'dp_1'}, dimensions={0}, use_global_device_ids=true | all-gather | bytes 10240 | tf_op jit(solution)/shard_map/all_gather | solution.py:79
  183.3 8.1 %all-gather.6 = f32[4,2,256]{2,1,0:T(2,128)S(1)} all-gather(f32[1,2,256]{2,1,0:T(2,128)S(1)} %maximum_bitcast_fusion.2), channel_id=4, replica_groups=mesh['dp_0'=4,'dp_1'=4,'mp_0'=4,'mp_1'=2] {'mp_0'}, dimensions={0}, use_global_device_ids=true | all-gather | bytes 10240 | tf_op jit(solution)/shard_map/all_gather | solution.py:79
  191.5 10.2 %all-gather.7 = f32[2,2,256]{2,1,0:T(2,128)S(1)} all-gather(f32[1,2,256]{2,1,0:T(2,128)S(1)} %maximum_bitcast_fusion.3), channel_id=5, replica_groups=mesh['dp_0'=4,'dp_1'=4,'mp_0'=4,'mp_1'=2] {'mp_1'}, dimensions={0}, use_global_device_ids=true | all-gather | bytes 6144 | tf_op jit(solution)/shard_map/all_gather | solution.py:79
  201.7 0.8 copy.74
  (48 shorter events, 1.0 us)
Async XLA Ops:
  0.0 162.9 %copy-start = (bf16[4096,125]{1,0:T(8,128)(2,1)S(1)}, bf16[4096,125]{1,0:T(8,128)(2,1)}, u32[]{:S(2)}) copy-start(bf16[4096,125]{1,0:T(8,128)(2,1)} %param.33) | copy-start | bytes 3072004
  6.0 24.5 %all-to-all-start = ((bf16[16,8,4096]{2,1,0:T(8,128)(2,1)}), bf16[16,8,4096]{2,1,0:T(8,128)(2,1)S(1)}, u32[]{:S(2)}, u32[]{:S(2)}) async-start(bf16[16,8,4096]{2,1,0:T(8,128)(2,1)} %broadcast_in_dim.24), calls=%async_computation | async-start | bytes 2097152 | tf_op jit(solution)/shard_map/all_to_all | solution.py:18
  34.8 14.6 %copy-start.3 = (bf16[2,128,1024]{2,1,0:T(8,128)(2,1)S(1)}, bf16[2,128,1024]{2,1,0:T(8,128)(2,1)}, u32[]{:S(2)}) copy-start(bf16[2,128,1024]{2,1,0:T(8,128)(2,1)} %param.31) | copy-start | bytes 1572868
  34.9 14.6 %copy-start.5 = (bf16[2,2,16,128]{3,2,1,0:T(8,128)(2,1)S(1)}, bf16[2,2,16,128]{3,2,1,0:T(8,128)(2,1)}, u32[]{:S(2)}) copy-start(bf16[2,2,16,128]{3,2,1,0:T(8,128)(2,1)} %param.29) | copy-start | bytes 49156
  43.5 48.8 %copy-start.4 = (bf16[2,16,1024]{2,1,0:T(8,128)(2,1)S(1)}, bf16[2,16,1024]{2,1,0:T(8,128)(2,1)}, u32[]{:S(2)}) copy-start(bf16[2,16,1024]{2,1,0:T(8,128)(2,1)} %param.26) | copy-start | bytes 196612
  43.5 49.0 %copy-start.7 = (f32[2,1024]{1,0:T(2,128)S(1)}, f32[2,1024]{1,0:T(2,128)}, u32[]{:S(2)}) copy-start(f32[2,1024]{1,0:T(2,128)} %param.32) | copy-start | bytes 24580
  43.5 63.9 %copy-start.2 = (bf16[16,4096]{1,0:T(8,128)(2,1)S(1)}, bf16[16,4096]{1,0:T(8,128)(2,1)}, u32[]{:S(2)}) copy-start(bf16[16,4096]{1,0:T(8,128)(2,1)} %param.18) | copy-start | bytes 393220
  43.5 64.1 %copy-start.6 = (f32[4096]{0:T(1024)S(1)}, f32[4096]{0:T(1024)}, u32[]{:S(2)}) copy-start(f32[4096]{0:T(1024)} %param.24) | copy-start | bytes 49156
  43.5 19.5 %all-to-all-start.1 = ((bf16[16,8,4096]{2,1,0:T(8,128)(2,1)}), bf16[16,8,4096]{2,1,0:T(8,128)(2,1)S(1)}, u32[]{:S(2)}, u32[]{:S(2)}) async-start(bf16[16,8,4096]{2,1,0:T(8,128)(2,1)} %fusion.9), calls=%async_computation.1 | async-start | bytes 2097152 | tf_op jit(solution)/shard_map/all_to_all | solution.py:44
  64.1 22.6 %all-to-all-start.3 = ((f32[8,2,16,1024]{3,2,1,0:T(8,128)}), f32[8,2,16,1024]{3,2,1,0:T(8,128)S(1)}, u32[]{:S(2)}, u32[]{:S(2)}) async-start(f32[8,2,16,1024]{3,2,1,0:T(8,128)} %broadcast_in_dim.29), calls=%async_computation.3 | async-start | bytes 2097152 | tf_op jit(solution)/shard_map/all_to_all | solution.py:18
  87.9 19.4 %all-to-all-start.2 = ((bf16[8,16,4096]{2,1,0:T(8,128)(2,1)}), bf16[8,16,4096]{2,1,0:T(8,128)(2,1)S(1)}, u32[]{:S(2)}, u32[]{:S(2)}) async-start(bf16[8,16,4096]{2,1,0:T(8,128)(2,1)} %broadcast_in_dim.25), calls=%async_computation.2 | async-start | bytes 2097152 | tf_op jit(solution)/shard_map/all_to_all | solution.py:18
  92.4 21.9 %copy-start.1 = (bf16[2,1024,125]{1,0,2:T(2,128)(2,1)S(1)}, bf16[2,1024,125]{1,0,2:T(2,128)(2,1)}, u32[]{:S(2)}) copy-start(bf16[2,1024,125]{1,0,2:T(2,128)(2,1)} %param.34) | copy-start | bytes 1536004
  109.8 51.3 %all-to-all-start.4 = ((bf16[16,16,6144]{2,1,0:T(8,128)(2,1)}), bf16[16,16,6144]{2,1,0:T(8,128)(2,1)}, u32[]{:S(2)}, u32[]{:S(2)}) async-start(bf16[16,16,6144]{2,1,0:T(8,128)(2,1)} %stack.5), calls=%async_computation.4 | async-start | bytes 6291456 | tf_op jit(solution)/shard_map/all_to_all | solution.py:60
  114.3 52.3 %copy-start.8 = (f32[256]{0:T(256)S(1)}, f32[256]{0:T(256)}, u32[]{:S(2)}) copy-start(f32[256]{0:T(256)} %param.35) | copy-start | bytes 3076
